TPU v7x, 256 devices: a whole 4x4x8 slice. The times are simulated.
256 devices in a mesh: ctx: 16 (over y_hi, z), tp: 8 (over x, y_lo), probe: 2 (over core).
Axes of the slice: x: 4, y: 4 (y_hi: 2, y_lo: 2; y = y_hi * 2 + y_lo), z: 8, core: 2. Of those that a mesh axis runs over, the one named last changes fastest.
Arguments:
- latent: float32 [2048, 3072], P('ctx', 'tp'), may hold values from -6 to 6
- probes: int32 [2, 2048, 3072], P('probe', 'ctx', 'tp'), may hold values from 0 to 1
- modulation: float32 [2, 3, 3072], replicated, may hold values from -3 to 3
- pattern: int32 [16, 8], P('ctx'), may hold values from 0 to 15, as said below
- w_qkv: bfloat16 [3072, 3, 3072], P(None, None, 'tp'), may hold values from -0.109375 to 0.109375
- w_out: bfloat16 [3072, 3072], P('tp'), may hold values from -0.109375 to 0.109375
- w_up: bfloat16 [3072, 6144], P('ctx', 'tp'), may hold values from -0.109375 to 0.109375
- w_down: bfloat16 [6144, 3072], P('tp', 'ctx'), may hold values from -0.078125 to 0.078125
- q_gain: float32 [3072], P('tp'), may hold values from 0.5 to 5.1, as said below
- k_gain: float32 [3072], P('tp'), may hold values from 0.5 to 2
Outputs:
- latent_out: float32 [2048, 3072], P('ctx', 'tp')
- density_change: float32 [2048], P('ctx')
Inputs may be any that keep to these rules, and one draw needn't show every extreme that they name: `pattern`: row q lists key blocks for query block q: its first entry is q; the next entries are distinct blocks other than q up to a count of 1 to 8, after which every entry is q again; row 0 lists 8 distinct blocks. `q_gain`: positive gains.
All inputs are finite; a program needn't handle non-finite values.
Results may differ from a plain program's by a relative error of at most 0.034.
Values may be sent and summed in bfloat16 or wider, within the bound.
A program may use at most 128 MiB of HBM per device.

v0:
```python
from functools import partial
import math
import jax
import jax.numpy as jnp
from jax import lax
from jax.sharding import PartitionSpec as P

HD = 128
BLK = 128
K_SEL = 8
STEPS = 2
EPS = 1e-06
NEG_BIG = -1e30


def norm_features(rows, tangent, shift, stretch, full_width):
    row_sums = jnp.stack(
        [jnp.sum(rows, 1), jnp.sum(rows * rows, 1), jnp.sum(tangent, 1), jnp.sum(rows * tangent, 1)]
    )
    totals = lax.psum(row_sums, "tp")
    row_mean = totals[0][:, None] / full_width
    row_var = totals[1][:, None] / full_width - row_mean * row_mean
    tan_mean = totals[2][:, None] / full_width
    tan_var = 2.0 * (totals[3][:, None] / full_width - row_mean * tan_mean)
    inv_std = lax.rsqrt(row_var + EPS)
    centred = rows - row_mean
    normed = centred * inv_std
    tan_normed = (
        tangent - tan_mean
    ) * inv_std - 0.5 * centred * inv_std * inv_std * inv_std * tan_var
    normed_act = (normed * (1.0 + stretch) + shift).astype(jnp.bfloat16)
    tangent_act = (tan_normed * (1.0 + stretch)).astype(jnp.bfloat16)
    return (
        lax.all_gather(normed_act, "tp", axis=1, tiled=True),
        lax.all_gather(tangent_act, "tp", axis=1, tiled=True),
    )


def head_rms(projected, tan_projected, head_gain):
    row_count = projected.shape[0]
    heads_local = head_gain.shape[0] // HD
    head_view = projected.reshape(row_count, heads_local, HD)
    tan_view = tan_projected.reshape(row_count, heads_local, HD)
    gain_view = head_gain.reshape(heads_local, HD)
    inv_std = lax.rsqrt(jnp.mean(head_view * head_view, axis=-1, keepdims=True) + EPS)
    tan_inv = -inv_std * inv_std * inv_std * jnp.mean(head_view * tan_view, axis=-1, keepdims=True)
    result = (head_view * inv_std * gain_view).astype(jnp.bfloat16)
    tan_result = ((tan_view * inv_std + head_view * tan_inv) * gain_view).astype(jnp.bfloat16)
    return (result, tan_result)


def empty_carry(heads_local, row_count):
    return (
        jnp.full((heads_local, row_count), NEG_BIG, jnp.float32),
        jnp.zeros((heads_local, row_count), jnp.float32),
        jnp.zeros((heads_local, row_count, HD), jnp.float32),
        jnp.zeros((heads_local, row_count, HD), jnp.float32),
        jnp.zeros((heads_local, row_count), jnp.float32),
    )


def attend(state_carry, query, key_set, allowed):
    running_max, run_total, run_acc, tan_acc, tan_sum = state_carry
    q_rows, dq_rows = query
    k_rows, v_rows, dk_rows, dv_rows = key_set
    score_scale = 1.0 / math.sqrt(q_rows.shape[2])
    scores = (
        jnp.einsum("qhd,khd->hqk", q_rows, k_rows, preferred_element_type=jnp.float32) * score_scale
    )
    tan_scores = (
        jnp.einsum("qhd,khd->hqk", dq_rows, k_rows, preferred_element_type=jnp.float32)
        + jnp.einsum("qhd,khd->hqk", q_rows, dk_rows, preferred_element_type=jnp.float32)
    ) * score_scale
    key_mask = allowed[None, :, :]
    scores = jnp.where(key_mask, scores, NEG_BIG)
    new_max = jnp.maximum(running_max, jnp.max(scores, axis=2))
    weights = jnp.where(key_mask, jnp.exp(scores - new_max[:, :, None]), 0.0)
    values = v_rows.astype(jnp.float32)
    tan_values = dv_rows.astype(jnp.float32)
    weighted_ds = weights * tan_scores
    run_total = jnp.sum(weights, axis=2)
    run_acc = jnp.einsum("hqk,khd->hqd", weights, values, precision=lax.Precision.HIGHEST)
    tan_acc = jnp.einsum(
        "hqk,khd->hqd", weights, tan_values, precision=lax.Precision.HIGHEST
    ) + jnp.einsum("hqk,khd->hqd", weighted_ds, values, precision=lax.Precision.HIGHEST)
    tan_sum = jnp.sum(weighted_ds, axis=2)
    return (new_max, run_total, run_acc, tan_acc, tan_sum)


def finish(state_carry):
    running_max, run_total, run_acc, tan_acc, tan_sum = state_carry
    output = run_acc / run_total[:, :, None]
    tan_output = tan_acc / run_total[:, :, None] - (tan_sum / run_total)[:, :, None] * output
    heads_local, row_count, head_size = output.shape
    output = (
        output.transpose(1, 0, 2).reshape(row_count, heads_local * head_size).astype(jnp.bfloat16)
    )
    tan_output = (
        tan_output.transpose(1, 0, 2)
        .reshape(row_count, heads_local * head_size)
        .astype(jnp.bfloat16)
    )
    return (output, tan_output)


def select_blocks(whole_rows, chosen, block_total, heads_local):
    blocked = whole_rows.reshape(block_total, BLK, heads_local * HD)
    return jnp.take(blocked, chosen, axis=0).reshape(K_SEL * BLK, heads_local, HD)


def listed_attention(q_rows, dq_rows, whole_set, pattern, block_total, heads_local):
    chosen = pattern[0]
    valid_cols = (jnp.arange(K_SEL) == 0) | (chosen != chosen[0])
    allowed = jnp.broadcast_to(jnp.repeat(valid_cols, BLK)[None, :], (BLK, K_SEL * BLK))
    key_set = tuple(
        (select_blocks(member, chosen, block_total, heads_local) for member in whole_set)
    )
    query = (q_rows[0:BLK], dq_rows[0:BLK])
    block_out, block_tan = finish(attend(empty_carry(heads_local, BLK), query, key_set, allowed))
    return (block_out, block_tan)


def local(latent, probes, modulation, pattern, w_qkv, w_out, w_up, w_down, q_gain, k_gain):
    row_count, local_width = latent.shape
    full_width = local_width * lax.axis_size("tp")
    feature_start = lax.axis_index("tp") * local_width
    heads_local = q_gain.shape[0] // HD
    block_total = row_count * lax.axis_size("ctx") // BLK
    step_size = 1.0 / STEPS
    probe_signs = 2.0 * probes[0].astype(jnp.float32) - 1.0
    up_full, down_full = (
        lax.all_gather(w_up, "ctx", axis=0, tiled=True),
        lax.all_gather(w_down, "ctx", axis=1, tiled=True),
    )
    gelu_tanh = partial(jax.nn.gelu, approximate=True)
    change = jnp.zeros((row_count,), jnp.float32)
    for euler_step in range(STEPS):
        mod_local = lax.dynamic_slice_in_dim(modulation[euler_step], feature_start, local_width, 1)
        normed_act, tangent_act = norm_features(
            latent, probe_signs, mod_local[0], mod_local[1], full_width
        )
        stacked = jnp.concatenate([normed_act, tangent_act], axis=0)
        projected = jnp.einsum("rd,dcf->crf", stacked, w_qkv, preferred_element_type=jnp.float32)
        q_rows, dq_rows = head_rms(projected[0, :row_count], projected[0, row_count:], q_gain)
        k_heads, dk_heads = head_rms(projected[1, :row_count], projected[1, row_count:], k_gain)
        k_rows = k_heads.reshape(row_count, heads_local * HD)
        dk_rows = dk_heads.reshape(row_count, heads_local * HD)
        v_rows = projected[2, :row_count].astype(jnp.bfloat16)
        dv_rows = projected[2, row_count:].astype(jnp.bfloat16)
        k_whole, v_whole, dk_whole, dv_whole = (
            lax.all_gather(k_rows, "ctx", axis=0, tiled=True),
            lax.all_gather(v_rows, "ctx", axis=0, tiled=True),
            lax.all_gather(dk_rows, "ctx", axis=0, tiled=True),
            lax.all_gather(dv_rows, "ctx", axis=0, tiled=True),
        )
        attended, tan_attended = listed_attention(
            q_rows,
            dq_rows,
            (k_whole, v_whole, dk_whole, dv_whole),
            pattern,
            block_total,
            heads_local,
        )
        pre_hidden = jnp.dot(stacked, up_full, preferred_element_type=jnp.float32)
        hidden, tan_hidden = jax.jvp(
            gelu_tanh, (pre_hidden[:row_count],), (pre_hidden[row_count:],)
        )
        attn_rows = jnp.concatenate([attended, tan_attended], axis=0)
        mlp_rows = jnp.concatenate(
            [hidden.astype(jnp.bfloat16), tan_hidden.astype(jnp.bfloat16)], axis=0
        )
        partials = jnp.dot(attn_rows, w_out, preferred_element_type=jnp.float32) + jnp.dot(
            mlp_rows, down_full, preferred_element_type=jnp.float32
        )
        summed = lax.psum_scatter(
            partials.astype(jnp.bfloat16), "tp", scatter_dimension=1, tiled=True
        ).astype(jnp.float32)
        speed = mod_local[2] * summed[:row_count]
        tan_speed = mod_local[2] * summed[row_count:]
        change = change + jnp.sum(probe_signs * tan_speed, axis=1)
        latent = latent + step_size * speed
    total_change = lax.psum(change, ("tp", "probe"))
    density_change = -step_size * total_change / (lax.axis_size("probe") * math.sqrt(full_width))
    return (latent, density_change)


def solution(mesh):
    return jax.shard_map(
        local,
        mesh=mesh,
        in_specs=(
            P("ctx", "tp"),
            P("probe", "ctx", "tp"),
            P(),
            P("ctx", None),
            P(None, None, "tp"),
            P("tp", None),
            P("ctx", "tp"),
            P("tp", "ctx"),
            P("tp"),
            P("tp"),
        ),
        out_specs=(P("ctx", "tp"), P("ctx")),
        check_vma=False,
    )
```

profile of v0, /device:TPU:1, one launch (start us, length us, event | category | flops | bytes accessed | tf_op | source)
XLA Modules:
  0.0 1214.0 jit_solution(16724503533342251219)
XLA Ops:
  9.6 16.8 %psum.21 = f32[4,128]{1,0:T(4,128)S(1)} all-reduce(f32[4,128]{1,0:T(4,128)S(1)} %fusion.105), channel_id=1, replica_groups=mesh['ctx'=16,'tp'=8,'probe'=2] {'tp'}, use_global_device_ids=true, to_apply=%region_4.0 | all-reduce | flops 512 | bytes 4096 | tf_op jit(solution)/shard_map/psum | solution.py:20
  26.4 1.6 fusion.134
  29.3 25.0 %all_gather.43 = bf16[128,3072]{1,0:T(8,128)(2,1)S(1)} all-gather(bf16[128,384]{1,0:T(8,128)(2,1)S(1)} %get-tuple-element.49), channel_id=1, replica_groups=mesh['ctx'=16,'tp'=8,'probe'=2] {'tp'}, dimensions={1}, use_global_device_ids=true | all-gather | bytes 884736 | tf_op jit(solution)/shard_map/all_gather | solution.py:35
  54.4 24.5 %all_gather.42 = bf16[128,3072]{1,0:T(8,128)(2,1)S(1)} all-gather(bf16[128,384]{1,0:T(8,128)(2,1)S(1)} %get-tuple-element.50), channel_id=1, replica_groups=mesh['ctx'=16,'tp'=8,'probe'=2] {'tp'}, dimensions={1}, use_global_device_ids=true | all-gather | bytes 884736 | tf_op jit(solution)/shard_map/all_gather | solution.py:34
  79.0 5.8 fusion.135
  87.3 1.8 copy.102
  89.0 1.7 copy.91
  91.7 1.5 reduce_sum.202
  94.6 1.7 copy.103
  97.0 1.7 copy.92
  98.8 1.7 fusion.83
  105.8 74.2 %all-gather.27.cloned.1.call-done = bf16[1,2048,384]{2,1,0:T(8,128)(2,1)} async-done(((bf16[1,128,384]{2,1,0:T(8,128)(2,1)}), bf16[1,2048,384]{2,1,0:T(8,128)(2,1)}) %all-gather.27.cloned.1.call-update) | async-done | bytes 1572880 | tf_op jit(solution)/shard_map/all_gather | solution.py:152
  180.0 2.1 gather_fusion.1
  182.1 79.4 %all-gather.29.cloned.1.call-done = bf16[1,2048,384]{2,1,0:T(8,128)(2,1)} async-done(((bf16[1,128,384]{2,1,0:T(8,128)(2,1)}), bf16[1,2048,384]{2,1,0:T(8,128)(2,1)}) %all-gather.29.cloned.1.call-update) | async-done | bytes 1572880 | tf_op jit(solution)/shard_map/all_gather | solution.py:154
  261.5 3.0 gather_fusion.2
  264.5 79.1 %all-gather.17.cloned.1.call-done = bf16[2048,384]{1,0:T(8,128)(2,1)} async-done(((bf16[128,384]{1,0:T(8,128)(2,1)}), bf16[2048,384]{1,0:T(8,128)(2,1)}) %all-gather.17.cloned.1.call-update) | async-done | bytes 1572880 | tf_op jit(solution)/shard_map/all_gather | solution.py:153
  343.6 2.9 gather_fusion.3
  346.5 78.4 %all-gather.15.cloned.1.call-done = bf16[2048,384]{1,0:T(8,128)(2,1)} async-done(((bf16[128,384]{1,0:T(8,128)(2,1)}), bf16[2048,384]{1,0:T(8,128)(2,1)}) %all-gather.15.cloned.1.call-update) | async-done | bytes 1572880 | tf_op jit(solution)/shard_map/all_gather | solution.py:151
  424.9 3.0 gather_fusion
  427.9 3.4 broadcast_select_fusion.6
  431.4 1.6 copy.96
  433.0 1.2 reshape.365
  434.2 2.5 copy.97
  436.8 2.2 reshape.367
  438.9 1.4 copy.93
  440.3 1.4 reshape.363
  441.7 3.2 reshape.476
  451.8 76.6 %all-gather.19.cloned.1.call-done = bf16[3072,768]{1,0:T(8,128)(2,1)} async-done(((bf16[192,768]{1,0:T(8,128)(2,1)}), bf16[3072,768]{1,0:T(8,128)(2,1)}) %all-gather.19.cloned.1.call-update) | async-done | bytes 4718608 | tf_op jit(solution)/shard_map/all_gather | solution.py:132
  528.4 4.2 fusion.143
  532.9 98.5 %all-gather.21.cloned.1.call-done = bf16[768,3072]{0,1:T(8,128)(2,1)} async-done(((bf16[768,192]{0,1:T(8,128)(2,1)}), bf16[768,3072]{0,1:T(8,128)(2,1)}) %all-gather.21.cloned.1.call-update) | async-done | bytes 4718608 | tf_op jit(solution)/shard_map/all_gather | solution.py:133
  631.3 3.7 fusion.54
  635.1 2.2 fusion
  637.2 2.6 copy.142
  639.9 1.4 dynamic-slice_reduce_fusion.1
  641.3 42.1 %reduce-scatter.7.cloned.1.call-done = bf16[384,256]{1,0:T(8,128)(2,1)} async-done(((bf16[3072,256]{1,0:T(8,128)(2,1)}), bf16[384,256]{1,0:T(8,128)(2,1)}) %reduce-scatter.7.cloned.1.call-update) | async-done | bytes 196624
  684.7 14.6 %psum.22 = f32[4,128]{1,0:T(4,128)S(1)} all-reduce(f32[4,128]{1,0:T(4,128)S(1)} %fusion.106), channel_id=1, replica_groups=mesh['ctx'=16,'tp'=8,'probe'=2] {'tp'}, use_global_device_ids=true, to_apply=%region_16.18 | all-reduce | flops 512 | bytes 4096 | tf_op jit(solution)/shard_map/psum | solution.py:20
  699.6 24.3 %all_gather.51 = bf16[128,3072]{1,0:T(8,128)(2,1)S(1)} all-gather(bf16[128,384]{1,0:T(8,128)(2,1)S(1)} %get-tuple-element.47), channel_id=1, replica_groups=mesh['ctx'=16,'tp'=8,'probe'=2] {'tp'}, dimensions={1}, use_global_device_ids=true | all-gather | bytes 884736 | tf_op jit(solution)/shard_map/all_gather | solution.py:35
  723.8 24.5 %all_gather.50 = bf16[128,3072]{1,0:T(8,128)(2,1)S(1)} all-gather(bf16[128,384]{1,0:T(8,128)(2,1)S(1)} %get-tuple-element.48), channel_id=1, replica_groups=mesh['ctx'=16,'tp'=8,'probe'=2] {'tp'}, dimensions={1}, use_global_device_ids=true | all-gather | bytes 884736 | tf_op jit(solution)/shard_map/all_gather | solution.py:34
  748.4 6.8 fusion.139
  756.8 2.0 slice_multiply_fusion.4
  759.4 1.8 fusion.78
  763.9 4.3 fusion.144
  768.6 3.1 fusion.58
  771.6 79.8 %all-gather.31.cloned.1.call-done = bf16[1,2048,384]{2,1,0:T(8,128)(2,1)} async-done(((bf16[1,128,384]{2,1,0:T(8,128)(2,1)}), bf16[1,2048,384]{2,1,0:T(8,128)(2,1)}) %all-gather.31.cloned.1.call-update) | async-done | bytes 1572880 | tf_op jit(solution)/shard_map/all_gather | solution.py:152
  851.4 2.2 gather_fusion.5
  853.6 79.3 %all-gather.33.cloned.1.call-done = bf16[1,2048,384]{2,1,0:T(8,128)(2,1)} async-done(((bf16[1,128,384]{2,1,0:T(8,128)(2,1)}), bf16[1,2048,384]{2,1,0:T(8,128)(2,1)}) %all-gather.33.cloned.1.call-update) | async-done | bytes 1572880 | tf_op jit(solution)/shard_map/all_gather | solution.py:154
  932.9 3.1 gather_fusion.6
  936.0 78.3 %all-gather.25.cloned.1.call-done = bf16[2048,384]{1,0:T(8,128)(2,1)} async-done(((bf16[128,384]{1,0:T(8,128)(2,1)}), bf16[2048,384]{1,0:T(8,128)(2,1)}) %all-gather.25.cloned.1.call-update) | async-done | bytes 1572880 | tf_op jit(solution)/shard_map/all_gather | solution.py:153
  1014.2 3.1 gather_fusion.7
  1017.3 78.4 %all-gather.23.cloned.1.call-done = bf16[2048,384]{1,0:T(8,128)(2,1)} async-done(((bf16[128,384]{1,0:T(8,128)(2,1)}), bf16[2048,384]{1,0:T(8,128)(2,1)}) %all-gather.23.cloned.1.call-update) | async-done | bytes 1572880 | tf_op jit(solution)/shard_map/all_gather | solution.py:151
  1095.8 3.1 gather_fusion.4
  1098.8 3.5 broadcast_select_fusion.2
  1102.3 2.5 copy.113
  1104.9 2.2 reshape.373
  1107.0 1.3 copy.110
  1108.4 1.4 reshape.371
  1109.8 2.4 copy.114
  1112.2 2.2 reshape.375
  1114.4 3.2 reshape.477
  1124.2 2.2 fusion.1
  1126.4 2.6 copy.144
  1129.1 44.3 %reduce-scatter.9.cloned.1.call-done = bf16[384,256]{1,0:T(8,128)(2,1)} async-done(((bf16[3072,256]{1,0:T(8,128)(2,1)}), bf16[384,256]{1,0:T(8,128)(2,1)}) %reduce-scatter.9.cloned.1.call-update) | async-done | bytes 196624
  1174.5 1.7 fusion.63
  1176.2 30.4 %psum.23 = f32[128]{0:T(128)S(1)} all-reduce(f32[128]{0:T(128)S(1)} %add.227), channel_id=1, replica_groups=mesh['ctx'=16,'tp'=8,'probe'=2] {'tp','probe'}, use_global_device_ids=true, to_apply=%region_27.29 | all-reduce | flops 128 | bytes 1024 | tf_op jit(solution)/shard_map/psum | solution.py:182
  (157 shorter events, 36.3 us)
Async XLA Ops:
  7.2 627.9 %copy-start = (bf16[384,3072]{1,0:T(8,128)(2,1)S(1)}, bf16[384,3072]{1,0:T(8,128)(2,1)}, u32[]{:S(2)}) copy-start(bf16[384,3072]{1,0:T(8,128)(2,1)} %param.17) | copy-start | bytes 7077892
  7.2 172.8 %all-gather.27.cloned.1.call-start = ((), (), s32[]{:S(2)}) async-start(), calls=%async_computation.8 | async-start | bytes 1671168 | tf_op jit(solution)/shard_map/all_gather | solution.py:152
  8.4 1.2 copy-start.26
  79.0 5.8 copy-start.17
  85.6 175.9 %all-gather.29.cloned.1.call-start = ((), (), s32[]{:S(2)}) async-start(), calls=%async_computation.9 | async-start | bytes 1671168 | tf_op jit(solution)/shard_map/all_gather | solution.py:154
  86.3 257.3 %all-gather.17.cloned.1.call-start = ((), (), s32[]{:S(2)}) async-start(), calls=%async_computation.3 | async-start | bytes 1671168 | tf_op jit(solution)/shard_map/all_gather | solution.py:153
  87.3 11.5 copy-start.21
  96.3 8.1 copy-start.28
  100.5 324.4 %all-gather.15.cloned.1.call-start = ((), (), s32[]{:S(2)}) async-start(), calls=%async_computation.2 | async-start | bytes 1671168 | tf_op jit(solution)/shard_map/all_gather | solution.py:151
  101.1 427.2 %all-gather.19.cloned.1.call-start = ((), (), s32[]{:S(2)}) async-start(), calls=%async_computation.4 | async-start | bytes 5013504 | tf_op jit(solution)/shard_map/all_gather | solution.py:132
  101.7 529.6 %all-gather.21.cloned.1.call-start = ((), (), s32[]{:S(2)}) async-start(), calls=%async_computation.5 | async-start | bytes 5013504 | tf_op jit(solution)/shard_map/all_gather | solution.py:133
  102.3 581.1 %reduce-scatter.7.cloned.1.call-start = ((), (), s32[]{:S(2)}) async-start(), calls=%async_computation.12 | async-start | bytes 1769472
  104.5 320.5 %copy-start.20 = (s32[1024]{0:T(1024)}, s32[1024]{0:T(1024)S(1)}, u32[]{:S(2)}) copy-start(s32[1024]{0:T(1024)S(1)} %pad_clamp_fusion) | copy-start | bytes 12292
  434.2 4.7 copy-start.5
  440.3 4.7 copy-start.19
  445.0 1.0 copy-start.25
  446.0 1.2 copy-start.4
  447.2 1.1 copy-start.15
  448.1 1.5 copy-start.8
  639.8 44.7 %copy-start.2 = (s32[1,128,384]{2,1,0:T(8,128)S(1)}, s32[1,128,384]{2,1,0:T(8,128)}, u32[]{:S(2)}) copy-start(s32[1,128,384]{2,1,0:T(8,128)} %param.13) | copy-start | bytes 589828
  639.8 44.7 %copy-start.11 = (f32[128,384]{1,0:T(8,128)S(1)}, f32[128,384]{1,0:T(8,128)}, u32[]{:S(2)}) copy-start(f32[128,384]{1,0:T(8,128)} %param.12) | copy-start | bytes 589828
  639.8 44.9 %copy-start.27 = (f32[128]{0:T(128)S(1)}, f32[128]{0:T(128)}, u32[]{:S(2)}) copy-start(f32[128]{0:T(128)} %copy-done.26) | copy-start | bytes 1540
  639.9 211.5 %all-gather.31.cloned.1.call-start = ((), (), s32[]{:S(2)}) async-start(), calls=%async_computation.10 | async-start | bytes 1671168 | tf_op jit(solution)/shard_map/all_gather | solution.py:152
  684.5 63.8 %copy-start.14 = (f32[256,384]{1,0:T(8,128)}, f32[256,384]{1,0:T(8,128)S(1)}, u32[]{:S(2)}) copy-start(f32[256,384]{1,0:T(8,128)S(1)} %convert_element_type.128) | copy-start | bytes 1179652
  684.7 63.6 %copy-start.12 = (f32[128,384]{1,0:T(8,128)}, f32[128,384]{1,0:T(8,128)S(1)}, u32[]{:S(2)}) copy-start(f32[128,384]{1,0:T(8,128)S(1)} %get-tuple-element.23) | copy-start | bytes 589828
  748.4 6.8 copy-start.18
  756.0 176.9 %all-gather.33.cloned.1.call-start = ((), (), s32[]{:S(2)}) async-start(), calls=%async_computation.11 | async-start | bytes 1671168 | tf_op jit(solution)/shard_map/all_gather | solution.py:154
  756.7 257.5 %all-gather.25.cloned.1.call-start = ((), (), s32[]{:S(2)}) async-start(), calls=%async_computation.7 | async-start | bytes 1671168 | tf_op jit(solution)/shard_map/all_gather | solution.py:153
  758.7 0.7 copy-start.22
  761.2 334.6 %all-gather.23.cloned.1.call-start = ((), (), s32[]{:S(2)}) async-start(), calls=%async_computation.6 | async-start | bytes 1671168 | tf_op jit(solution)/shard_map/all_gather | solution.py:151
  761.9 411.4 %reduce-scatter.9.cloned.1.call-start = ((), (), s32[]{:S(2)}) async-start(), calls=%async_computation.13 | async-start | bytes 1769472
  762.1 6.2 copy-start.9
  762.1 6.4 slice-start
  763.9 4.7 slice-start.1
  1102.3 4.7 copy-start.6
  1117.6 0.9 copy-start.10
  1117.6 0.9 copy-start.24
  1118.6 1.1 copy-start.16
  1119.7 1.2 copy-start.3
  1120.9 1.1 copy-start.7
  1122.1 2.1 copy-start.1
  1129.0 45.4 %copy-start.13 = (f32[128,384]{1,0:T(8,128)S(1)}, f32[128,384]{1,0:T(8,128)}, u32[]{:S(2)}) copy-start(f32[128,384]{1,0:T(8,128)} %copy-done.12) | copy-start | bytes 589828
  1129.0 45.4 %copy-start.23 = (f32[384]{0:T(512)S(1)}, f32[384]{0:T(512)}, u32[]{:S(2)}) copy-start(f32[384]{0:T(512)} %get-tuple-element.15) | copy-start | bytes 4612
Sparse Core Ops, SparseCore 0:
  85.7 94.2 all-gather.26
  182.6 78.8 all-gather.28
  264.7 78.8 all-gather.16
  346.0 78.8 all-gather.14
  427.4 100.9 all-gather.18
  530.8 100.4 all-gather.20
  640.0 43.3 reduce-scatter.6
  756.1 95.2 all-gather.30
  854.0 78.8 all-gather.32
  935.3 78.8 all-gather.24
  1016.8 78.8 all-gather.22
  1129.2 44.1 reduce-scatter.8
where the time goes:
time: 1220 us; the launch traced here: 1210 us
  waiting for transfers between devices  892 us (73%)
  blocking collectives  160 us (13%)
  local copies, waits for them, and re-layouts  76.3 us (6%)
  matrix products  42.8 us (4%)
  other arithmetic  27.4 us (2%)
  between operations  14.8 us (1%)
    all_gather x2, waiting for transfers between devices, local(): lax.all_gather(dv_rows, 'ctx', axis=0, tiled=True)  159 us
    all_gather x2, waiting for transfers between devices, local(): lax.all_gather(dk_rows, 'ctx', axis=0, tiled=True)  157 us
    all_gather x2, waiting for transfers between devices, local(): lax.all_gather(k_rows, 'ctx', axis=0, tiled=True)  157 us
    all_gather x2, waiting for transfers between devices, local(): lax.all_gather(v_rows, 'ctx', axis=0, tiled=True)  154 us
    all_gather x1, waiting for transfers between devices, local(): lax.all_gather(w_down, 'ctx', axis=1, tiled=True)  98.5 us
    unnamed x14, waiting for transfers between devices  90.1 us
    all_gather x1, waiting for transfers between devices, local(): lax.all_gather(w_up, 'ctx', axis=0, tiled=True)  76.6 us
    all_gather x2, blocking collectives, norm_features(): lax.all_gather(tangent_act, 'tp', axis=1, tiled=True)  49.3 us
  transfers between devices with their start and end apart: 12, of which 12 were waited for; matrix products, arithmetic and copies ran while one was open for 7% of the time, Pallas kernels for 0%

commit v1 on v0

--- a/solution.py
+++ b/solution.py
@@ -179,7 +179,8 @@
         tan_speed = mod_local[2] * summed[row_count:]
         change = change + jnp.sum(probe_signs * tan_speed, axis=1)
         latent = latent + step_size * speed
-    total_change = lax.psum(change, ("tp", "probe"))
+    half = lax.psum(change, "probe")
+    total_change = lax.psum(half, "tp")
     density_change = -step_size * total_change / (lax.axis_size("probe") * math.sqrt(full_width))
     return (latent, density_change)
 

time: 1220 us -> 1210 us (level)
    psum x1 -> x2, blocking collectives: 30.4 us -> 20 us  [the longest x1 14.3 us: local(): total_change = lax.psum(half, 'tp')]
where the time goes in v1:
time: 1210 us; the launch traced here: 1200 us
  waiting for transfers between devices  893 us (74%)
  blocking collectives  150 us (12%)
  local copies, waits for them, and re-layouts  76.3 us (6%)
  matrix products  42.8 us (4%)
  other arithmetic  27.5 us (2%)
  between operations  14.8 us (1%)
    all_gather x2, waiting for transfers between devices, local(): lax.all_gather(dv_rows, 'ctx', axis=0, tiled=True)  159 us
    all_gather x2, waiting for transfers between devices, local(): lax.all_gather(dk_rows, 'ctx', axis=0, tiled=True)  157 us
    all_gather x2, waiting for transfers between devices, local(): lax.all_gather(k_rows, 'ctx', axis=0, tiled=True)  157 us
    all_gather x2, waiting for transfers between devices, local(): lax.all_gather(v_rows, 'ctx', axis=0, tiled=True)  154 us
    all_gather x1, waiting for transfers between devices, local(): lax.all_gather(w_down, 'ctx', axis=1, tiled=True)  98.5 us
    unnamed x14, waiting for transfers between devices  90.3 us
    all_gather x1, waiting for transfers between devices, local(): lax.all_gather(w_up, 'ctx', axis=0, tiled=True)  76.6 us
    all_gather x2, blocking collectives, norm_features(): lax.all_gather(tangent_act, 'tp', axis=1, tiled=True)  49.3 us
  transfers between devices with their start and end apart: 12, of which 12 were waited for; matrix products, arithmetic and copies ran while one was open for 7% of the time, Pallas kernels for 0%

profile of v1, /device:TPU:1, one launch (start us, length us, event | category | flops | bytes accessed | tf_op | source)
XLA Modules:
  0.0 1204.0 jit_solution(18139537616674505476)
XLA Ops:
  9.6 16.8 %psum.28 = f32[4,128]{1,0:T(4,128)S(1)} all-reduce(f32[4,128]{1,0:T(4,128)S(1)} %fusion.105), channel_id=1, replica_groups=mesh['ctx'=16,'tp'=8,'probe'=2] {'tp'}, use_global_device_ids=true, to_apply=%region_4.0 | all-reduce | flops 512 | bytes 4096 | tf_op jit(solution)/shard_map/psum | solution.py:20
  26.4 1.6 fusion.134
  29.3 25.0 %all_gather.43 = bf16[128,3072]{1,0:T(8,128)(2,1)S(1)} all-gather(bf16[128,384]{1,0:T(8,128)(2,1)S(1)} %get-tuple-element.49), channel_id=1, replica_groups=mesh['ctx'=16,'tp'=8,'probe'=2] {'tp'}, dimensions={1}, use_global_device_ids=true | all-gather | bytes 884736 | tf_op jit(solution)/shard_map/all_gather | solution.py:35
  54.3 24.5 %all_gather.42 = bf16[128,3072]{1,0:T(8,128)(2,1)S(1)} all-gather(bf16[128,384]{1,0:T(8,128)(2,1)S(1)} %get-tuple-element.50), channel_id=1, replica_groups=mesh['ctx'=16,'tp'=8,'probe'=2] {'tp'}, dimensions={1}, use_global_device_ids=true | all-gather | bytes 884736 | tf_op jit(solution)/shard_map/all_gather | solution.py:34
  79.0 5.8 fusion.135
  87.3 1.7 copy.102
  89.0 1.7 copy.91
  91.7 1.5 reduce_sum.202
  94.6 1.7 copy.103
  97.0 1.7 copy.92
  98.8 1.7 fusion.83
  105.8 74.3 %all-gather.27.cloned.1.call-done = bf16[1,2048,384]{2,1,0:T(8,128)(2,1)} async-done(((bf16[1,128,384]{2,1,0:T(8,128)(2,1)}), bf16[1,2048,384]{2,1,0:T(8,128)(2,1)}) %all-gather.27.cloned.1.call-update) | async-done | bytes 1572880 | tf_op jit(solution)/shard_map/all_gather | solution.py:152
  180.0 2.1 gather_fusion.1
  182.1 79.4 %all-gather.29.cloned.1.call-done = bf16[1,2048,384]{2,1,0:T(8,128)(2,1)} async-done(((bf16[1,128,384]{2,1,0:T(8,128)(2,1)}), bf16[1,2048,384]{2,1,0:T(8,128)(2,1)}) %all-gather.29.cloned.1.call-update) | async-done | bytes 1572880 | tf_op jit(solution)/shard_map/all_gather | solution.py:154
  261.5 3.0 gather_fusion.2
  264.5 79.1 %all-gather.17.cloned.1.call-done = bf16[2048,384]{1,0:T(8,128)(2,1)} async-done(((bf16[128,384]{1,0:T(8,128)(2,1)}), bf16[2048,384]{1,0:T(8,128)(2,1)}) %all-gather.17.cloned.1.call-update) | async-done | bytes 1572880 | tf_op jit(solution)/shard_map/all_gather | solution.py:153
  343.6 3.0 gather_fusion.3
  346.5 78.4 %all-gather.15.cloned.1.call-done = bf16[2048,384]{1,0:T(8,128)(2,1)} async-done(((bf16[128,384]{1,0:T(8,128)(2,1)}), bf16[2048,384]{1,0:T(8,128)(2,1)}) %all-gather.15.cloned.1.call-update) | async-done | bytes 1572880 | tf_op jit(solution)/shard_map/all_gather | solution.py:151
  425.0 3.0 gather_fusion
  427.9 3.5 broadcast_select_fusion.6
  431.4 1.6 copy.96
  434.2 2.6 copy.97
  436.8 2.2 reshape.367
  439.0 1.4 copy.93
  440.3 1.4 reshape.363
  441.8 3.2 reshape.476
  451.8 76.6 %all-gather.19.cloned.1.call-done = bf16[3072,768]{1,0:T(8,128)(2,1)} async-done(((bf16[192,768]{1,0:T(8,128)(2,1)}), bf16[3072,768]{1,0:T(8,128)(2,1)}) %all-gather.19.cloned.1.call-update) | async-done | bytes 4718608 | tf_op jit(solution)/shard_map/all_gather | solution.py:132
  528.4 4.2 fusion.143
  532.9 98.5 %all-gather.21.cloned.1.call-done = bf16[768,3072]{0,1:T(8,128)(2,1)} async-done(((bf16[768,192]{0,1:T(8,128)(2,1)}), bf16[768,3072]{0,1:T(8,128)(2,1)}) %all-gather.21.cloned.1.call-update) | async-done | bytes 4718608 | tf_op jit(solution)/shard_map/all_gather | solution.py:133
  631.3 3.7 fusion.54
  635.1 2.1 fusion
  637.2 2.6 copy.142
  639.9 1.4 dynamic-slice_reduce_fusion.1
  641.3 42.1 %reduce-scatter.7.cloned.1.call-done = bf16[384,256]{1,0:T(8,128)(2,1)} async-done(((bf16[3072,256]{1,0:T(8,128)(2,1)}), bf16[384,256]{1,0:T(8,128)(2,1)}) %reduce-scatter.7.cloned.1.call-update) | async-done | bytes 196624
  684.8 14.6 %psum.29 = f32[4,128]{1,0:T(4,128)S(1)} all-reduce(f32[4,128]{1,0:T(4,128)S(1)} %fusion.106), channel_id=1, replica_groups=mesh['ctx'=16,'tp'=8,'probe'=2] {'tp'}, use_global_device_ids=true, to_apply=%region_16.18 | all-reduce | flops 512 | bytes 4096 | tf_op jit(solution)/shard_map/psum | solution.py:20
  699.6 24.3 %all_gather.51 = bf16[128,3072]{1,0:T(8,128)(2,1)S(1)} all-gather(bf16[128,384]{1,0:T(8,128)(2,1)S(1)} %get-tuple-element.47), channel_id=1, replica_groups=mesh['ctx'=16,'tp'=8,'probe'=2] {'tp'}, dimensions={1}, use_global_device_ids=true | all-gather | bytes 884736 | tf_op jit(solution)/shard_map/all_gather | solution.py:35
  723.8 24.3 %all_gather.50 = bf16[128,3072]{1,0:T(8,128)(2,1)S(1)} all-gather(bf16[128,384]{1,0:T(8,128)(2,1)S(1)} %get-tuple-element.48), channel_id=1, replica_groups=mesh['ctx'=16,'tp'=8,'probe'=2] {'tp'}, dimensions={1}, use_global_device_ids=true | all-gather | bytes 884736 | tf_op jit(solution)/shard_map/all_gather | solution.py:34
  748.3 6.8 fusion.139
  756.6 2.0 slice_multiply_fusion.4
  759.3 1.8 fusion.78
  763.8 4.3 fusion.144
  768.5 3.1 fusion.58
  771.5 80.1 %all-gather.31.cloned.1.call-done = bf16[1,2048,384]{2,1,0:T(8,128)(2,1)} async-done(((bf16[1,128,384]{2,1,0:T(8,128)(2,1)}), bf16[1,2048,384]{2,1,0:T(8,128)(2,1)}) %all-gather.31.cloned.1.call-update) | async-done | bytes 1572880 | tf_op jit(solution)/shard_map/all_gather | solution.py:152
  851.7 2.2 gather_fusion.5
  853.9 79.3 %all-gather.33.cloned.1.call-done = bf16[1,2048,384]{2,1,0:T(8,128)(2,1)} async-done(((bf16[1,128,384]{2,1,0:T(8,128)(2,1)}), bf16[1,2048,384]{2,1,0:T(8,128)(2,1)}) %all-gather.33.cloned.1.call-update) | async-done | bytes 1572880 | tf_op jit(solution)/shard_map/all_gather | solution.py:154
  933.2 3.1 gather_fusion.6
  936.2 78.3 %all-gather.25.cloned.1.call-done = bf16[2048,384]{1,0:T(8,128)(2,1)} async-done(((bf16[128,384]{1,0:T(8,128)(2,1)}), bf16[2048,384]{1,0:T(8,128)(2,1)}) %all-gather.25.cloned.1.call-update) | async-done | bytes 1572880 | tf_op jit(solution)/shard_map/all_gather | solution.py:153
  1014.5 3.1 gather_fusion.7
  1017.6 78.4 %all-gather.23.cloned.1.call-done = bf16[2048,384]{1,0:T(8,128)(2,1)} async-done(((bf16[128,384]{1,0:T(8,128)(2,1)}), bf16[2048,384]{1,0:T(8,128)(2,1)}) %all-gather.23.cloned.1.call-update) | async-done | bytes 1572880 | tf_op jit(solution)/shard_map/all_gather | solution.py:151
  1096.0 3.1 gather_fusion.4
  1099.1 3.5 broadcast_select_fusion.2
  1102.6 2.5 copy.113
  1105.2 2.2 reshape.373
  1107.3 1.3 copy.110
  1108.6 1.4 reshape.371
  1110.1 2.4 copy.114
  1112.5 2.2 reshape.375
  1114.7 3.2 reshape.477
  1124.5 2.2 fusion.1
  1126.7 2.6 copy.144
  1129.3 44.4 %reduce-scatter.9.cloned.1.call-done = bf16[384,256]{1,0:T(8,128)(2,1)} async-done(((bf16[3072,256]{1,0:T(8,128)(2,1)}), bf16[384,256]{1,0:T(8,128)(2,1)}) %reduce-scatter.9.cloned.1.call-update) | async-done | bytes 196624
  1174.9 1.7 fusion.63
  1176.6 5.7 psum.30
  1182.3 14.3 %psum.31 = f32[128]{0:T(128)S(1)} all-reduce(f32[128]{0:T(128)S(1)} %psum.30), channel_id=1, replica_groups=mesh['ctx'=16,'tp'=8,'probe'=2] {'tp'}, use_global_device_ids=true, to_apply=%region_28.30 | all-reduce | flops 128 | bytes 1024 | tf_op jit(solution)/shard_map/psum | solution.py:183
  (158 shorter events, 37.5 us)
Async XLA Ops:
  7.2 627.9 %copy-start = (bf16[384,3072]{1,0:T(8,128)(2,1)S(1)}, bf16[384,3072]{1,0:T(8,128)(2,1)}, u32[]{:S(2)}) copy-start(bf16[384,3072]{1,0:T(8,128)(2,1)} %param.17) | copy-start | bytes 7077892
  7.2 172.8 %all-gather.27.cloned.1.call-start = ((), (), s32[]{:S(2)}) async-start(), calls=%async_computation.8 | async-start | bytes 1671168 | tf_op jit(solution)/shard_map/all_gather | solution.py:152
  8.4 1.2 copy-start.26
  79.0 5.8 copy-start.17
  85.6 175.9 %all-gather.29.cloned.1.call-start = ((), (), s32[]{:S(2)}) async-start(), calls=%async_computation.9 | async-start | bytes 1671168 | tf_op jit(solution)/shard_map/all_gather | solution.py:154
  86.3 257.3 %all-gather.17.cloned.1.call-start = ((), (), s32[]{:S(2)}) async-start(), calls=%async_computation.3 | async-start | bytes 1671168 | tf_op jit(solution)/shard_map/all_gather | solution.py:153
  87.3 11.5 copy-start.21
  96.3 8.1 copy-start.28
  100.5 324.4 %all-gather.15.cloned.1.call-start = ((), (), s32[]{:S(2)}) async-start(), calls=%async_computation.2 | async-start | bytes 1671168 | tf_op jit(solution)/shard_map/all_gather | solution.py:151
  101.1 427.2 %all-gather.19.cloned.1.call-start = ((), (), s32[]{:S(2)}) async-start(), calls=%async_computation.4 | async-start | bytes 5013504 | tf_op jit(solution)/shard_map/all_gather | solution.py:132
  101.7 529.6 %all-gather.21.cloned.1.call-start = ((), (), s32[]{:S(2)}) async-start(), calls=%async_computation.5 | async-start | bytes 5013504 | tf_op jit(solution)/shard_map/all_gather | solution.py:133
  102.3 581.2 %reduce-scatter.7.cloned.1.call-start = ((), (), s32[]{:S(2)}) async-start(), calls=%async_computation.12 | async-start | bytes 1769472
  104.5 320.5 %copy-start.20 = (s32[1024]{0:T(1024)}, s32[1024]{0:T(1024)S(1)}, u32[]{:S(2)}) copy-start(s32[1024]{0:T(1024)S(1)} %pad_clamp_fusion) | copy-start | bytes 12292
  434.2 4.7 copy-start.5
  440.3 4.7 copy-start.19
  445.0 1.0 copy-start.25
  446.0 1.2 copy-start.4
  447.3 1.1 copy-start.15
  448.1 1.5 copy-start.8
  639.8 44.8 %copy-start.2 = (s32[1,128,384]{2,1,0:T(8,128)S(1)}, s32[1,128,384]{2,1,0:T(8,128)}, u32[]{:S(2)}) copy-start(s32[1,128,384]{2,1,0:T(8,128)} %param.13) | copy-start | bytes 589828
  639.8 44.8 %copy-start.11 = (f32[128,384]{1,0:T(8,128)S(1)}, f32[128,384]{1,0:T(8,128)}, u32[]{:S(2)}) copy-start(f32[128,384]{1,0:T(8,128)} %param.12) | copy-start | bytes 589828
  639.8 44.9 %copy-start.27 = (f32[128]{0:T(128)S(1)}, f32[128]{0:T(128)}, u32[]{:S(2)}) copy-start(f32[128]{0:T(128)} %copy-done.26) | copy-start | bytes 1540
  639.9 211.8 %all-gather.31.cloned.1.call-start = ((), (), s32[]{:S(2)}) async-start(), calls=%async_computation.10 | async-start | bytes 1671168 | tf_op jit(solution)/shard_map/all_gather | solution.py:152
  684.6 63.6 %copy-start.14 = (f32[256,384]{1,0:T(8,128)}, f32[256,384]{1,0:T(8,128)S(1)}, u32[]{:S(2)}) copy-start(f32[256,384]{1,0:T(8,128)S(1)} %convert_element_type.128) | copy-start | bytes 1179652
  684.8 63.5 %copy-start.12 = (f32[128,384]{1,0:T(8,128)}, f32[128,384]{1,0:T(8,128)S(1)}, u32[]{:S(2)}) copy-start(f32[128,384]{1,0:T(8,128)S(1)} %get-tuple-element.23) | copy-start | bytes 589828
  748.3 6.8 copy-start.18
  755.9 177.3 %all-gather.33.cloned.1.call-start = ((), (), s32[]{:S(2)}) async-start(), calls=%async_computation.11 | async-start | bytes 1671168 | tf_op jit(solution)/shard_map/all_gather | solution.py:154
  756.6 257.9 %all-gather.25.cloned.1.call-start = ((), (), s32[]{:S(2)}) async-start(), calls=%async_computation.7 | async-start | bytes 1671168 | tf_op jit(solution)/shard_map/all_gather | solution.py:153
  758.6 0.7 copy-start.22
  761.1 335.0 %all-gather.23.cloned.1.call-start = ((), (), s32[]{:S(2)}) async-start(), calls=%async_computation.6 | async-start | bytes 1671168 | tf_op jit(solution)/shard_map/all_gather | solution.py:151
  761.8 412.0 %reduce-scatter.9.cloned.1.call-start = ((), (), s32[]{:S(2)}) async-start(), calls=%async_computation.13 | async-start | bytes 1769472
  762.0 6.2 copy-start.9
  762.0 6.4 slice-start
  763.8 4.7 slice-start.1
  1102.6 4.7 copy-start.6
  1117.9 0.9 copy-start.10
  1117.9 0.9 copy-start.24
  1118.9 1.1 copy-start.16
  1120.0 1.2 copy-start.3
  1121.2 1.1 copy-start.7
  1122.3 2.1 copy-start.1
  1129.3 45.6 %copy-start.13 = (f32[128,384]{1,0:T(8,128)S(1)}, f32[128,384]{1,0:T(8,128)}, u32[]{:S(2)}) copy-start(f32[128,384]{1,0:T(8,128)} %copy-done.12) | copy-start | bytes 589828
  1129.3 45.6 %copy-start.23 = (f32[384]{0:T(512)S(1)}, f32[384]{0:T(512)}, u32[]{:S(2)}) copy-start(f32[384]{0:T(512)} %get-tuple-element.15) | copy-start | bytes 4612
Sparse Core Ops, SparseCore 0:
  85.7 94.2 all-gather.26
  182.6 78.8 all-gather.28
  264.7 78.8 all-gather.16
  346.0 78.8 all-gather.14
  427.4 100.9 all-gather.18
  530.8 100.4 all-gather.20
  640.0 43.4 reduce-scatter.6
  756.0 95.6 all-gather.30
  854.3 78.8 all-gather.32
  935.6 78.8 all-gather.24
  1017.1 78.8 all-gather.22
  1129.4 44.2 reduce-scatter.8
